TPU v7x, 8 devices: a whole 2x2x1 slice. The times are simulated.
8 devices in a mesh: rep: 1 (over z), dp: 8 (over x, y, core).
Axes of the slice: x: 2, y: 2, z: 1, core: 2. Of those that a mesh axis runs over, the one named last changes fastest.
Arguments:
- g_w_gate: bfloat16 [8, 2, 1152, 4608], P(('rep', 'dp'))
- g_w_up: bfloat16 [8, 2, 1152, 4608], P(('rep', 'dp'))
- g_w_down: bfloat16 [8, 2, 4608, 1152], P(('rep', 'dp'))
- w_gate: bfloat16 [2, 1152, 4608], replicated
- w_up: bfloat16 [2, 1152, 4608], replicated
- w_down: bfloat16 [2, 4608, 1152], replicated
- m_w_gate: float32 [2, 1152, 4608], P(None, 'dp')
- m_w_up: float32 [2, 1152, 4608], P(None, 'dp')
- m_w_down: float32 [2, 4608, 1152], P(None, 'dp')
- v_w_gate: float32 [2, 1152, 4608], P(None, 'dp')
- v_w_up: float32 [2, 1152, 4608], P(None, 'dp')
- v_w_down: float32 [2, 4608, 1152], P(None, 'dp')
Outputs:
- output 1: bfloat16 [2, 1152, 4608], P('rep')
- output 2: bfloat16 [2, 1152, 4608], P('rep')
- output 3: bfloat16 [2, 4608, 1152], P('rep')
- output 4: float32 [2, 1152, 4608], P('rep', 'dp')
- output 5: float32 [2, 1152, 4608], P('rep', 'dp')
- output 6: float32 [2, 4608, 1152], P('rep', 'dp')
- output 7: float32 [2, 1152, 4608], P('rep', 'dp')
- output 8: float32 [2, 1152, 4608], P('rep', 'dp')
- output 9: float32 [2, 4608, 1152], P('rep', 'dp')
All inputs are finite; a program needn't handle non-finite values.
Results may differ from a plain program's by a relative error of at most 0.022.
Values are sent between devices in bfloat16 or wider.
A program may use at most 2 GiB of HBM per device.

v0:
```python
import jax
import jax.numpy as jnp
from jax import lax
from jax.sharding import PartitionSpec as P


def adamw(w, m, v, g):
    m = 0.9 * m + 0.1 * g
    v = 0.95 * v + 0.05 * g * g
    step = m * lax.rsqrt(v + 1e-8) + 0.1 * w
    return (w - 0.02 * step).astype(jnp.bfloat16), m, v


def clipped(gradients, sum_of_squares, count):
    factor = jnp.minimum(1.0, 0.5 * lax.rsqrt(sum_of_squares / count + 1e-30))
    return [g * factor for g in gradients]


def solution(mesh):
    def step(*arrays):
        terms, weights, m, v = (arrays[i : i + 3] for i in (0, 3, 6, 9))
        gradients = [lax.psum_scatter(t[0], "dp", scatter_dimension=1, tiled=True).astype(jnp.float32) for t in terms]
        squares = lax.psum(sum(jnp.sum(g * g) for g in gradients), "dp")
        gradients = clipped(gradients, squares, lax.psum(1, "dp") * sum(g.size for g in gradients))
        me = lax.axis_index("dp")
        own = [lax.dynamic_slice_in_dim(w, me * one.shape[1], one.shape[1], 1).astype(jnp.float32) for w, one in zip(weights, m, strict=True)]
        new = [adamw(w, m, v, g) for w, m, v, g in zip(own, m, v, gradients, strict=True)]
        whole = [lax.all_gather(one[0], "dp", axis=1, tiled=True) for one in new]
        return (*whole, *(one[1] for one in new), *(one[2] for one in new))

    all_of, cut = P(None, None, None), P(None, "dp", None)
    return jax.shard_map(
        step,
        mesh=mesh,
        in_specs=(P(("rep", "dp"), None, None, None),) * 3 + (all_of,) * 3 + (cut,) * 6,
        out_specs=(P("rep", None, None),) * 3 + (P("rep", "dp", None),) * 6,
        check_vma=False,
    )
```

profile of v0, /device:TPU:0, one launch (start us, length us, event | category | flops | bytes accessed | tf_op | source)
XLA Modules:
  0.0 809.0 jit_solution(5215273503660967038)
XLA Ops:
  7.2 0.0 reduce-scatter.4.cloned.1.call-start
  7.2 0.7 reduce-scatter.4.cloned.1.call-update
  7.9 0.0 reduce-scatter.6.cloned.1.call-start
  8.0 0.7 reduce-scatter.6.cloned.1.call-update
  8.7 0.0 reduce-scatter.8.cloned.1.call-start
  8.7 0.7 reduce-scatter.8.cloned.1.call-update
  9.4 0.0 all-gather.8.cloned.1.call-start
  9.4 133.0 %reduce-scatter.4.cloned.1.call-done = bf16[2,144,4608]{2,1,0:T(8,128)(2,1)} async-done(((bf16[2,1152,4608]{2,1,0:T(8,128)(2,1)}), bf16[2,144,4608]{2,1,0:T(8,128)(2,1)}) %reduce-scatter.4.cloned.1.call-update) | async-done | bytes 2654224 | tf_op jit(solution)/shard_map/reduce_scatter | solution.py:22
  142.5 3.7 fusion.9
  146.2 127.9 %reduce-scatter.6.cloned.1.call-done = bf16[2,144,4608]{2,1,0:T(8,128)(2,1)} async-done(((bf16[2,1152,4608]{2,1,0:T(8,128)(2,1)}), bf16[2,144,4608]{2,1,0:T(8,128)(2,1)}) %reduce-scatter.6.cloned.1.call-update) | async-done | bytes 2654224 | tf_op jit(solution)/shard_map/reduce_scatter | solution.py:22
  274.1 3.7 fusion.10
  279.1 126.6 %reduce-scatter.8.cloned.1.call-done = bf16[2,576,1152]{2,1,0:T(8,128)(2,1)} async-done(((bf16[2,4608,1152]{2,1,0:T(8,128)(2,1)}), bf16[2,576,1152]{2,1,0:T(8,128)(2,1)}) %reduce-scatter.8.cloned.1.call-update) | async-done | bytes 2654224 | tf_op jit(solution)/shard_map/reduce_scatter | solution.py:22
  405.8 3.7 fusion.11
  410.1 22.2 %psum.7 = f32[]{:T(128)} all-reduce(f32[]{:T(128)S(6)} %add.65), channel_id=1, replica_groups=mesh['rep'=1,'dp'=8] {'dp'}, use_global_device_ids=true, to_apply=%region_6.0 | all-reduce | flops 1 | bytes 8 | tf_op jit(solution)/shard_map/psum | solution.py:23
  433.1 10.9 %fusion.17 = (bf16[2,576,1152]{2,1,0:T(8,128)(2,1)}, f32[2,576,1152]{2,1,0:T(8,128)}, f32[2,576,1152]{2,1,0:T(8,128)}) fusion(bf16[2,4608,1152]{2,1,0:T(8,128)(2,1)} %param.17, s32[]{:T(128)S(6)} %select_n.8, f32[]{:T(128)S(6)} %min_shard_map.3, bf16[2,576,1152]{2,1,0:T(8,128)(2,1)} %reduce-scatter.8.cloned.1.call-done, f32[2,576,1152]{2,1,0:T(8,128)} %param.23, ...), kind=kLoop, calls=%fused_computation.32 | loop fusion | flops 22560768 | bytes 29196296 | tf_op jit(solution)/shard_map/convert_element_type | solution.py:11
  443.9 0.0 all-gather.8.cloned.1.call-update
  444.0 0.0 all-gather.4.cloned.1.call-start
  444.0 0.0 copy-start.1
  444.0 10.9 %fusion.8 = (bf16[2,144,4608]{2,1,0:T(8,128)(2,1)}, f32[2,144,4608]{2,1,0:T(8,128)}, f32[2,144,4608]{2,1,0:T(8,128)}) fusion(bf16[2,1152,4608]{2,1,0:T(8,128)(2,1)} %param.15, s32[]{:T(128)S(6)} %select_n.7, f32[]{:T(128)S(6)} %min_shard_map.3, bf16[2,144,4608]{2,1,0:T(8,128)(2,1)} %reduce-scatter.4.cloned.1.call-done, f32[2,144,4608]{2,1,0:T(8,128)} %param.21, ...), kind=kLoop, calls=%fused_computation.23 | loop fusion | flops 22560768 | bytes 29196296 | tf_op jit(solution)/shard_map/convert_element_type | solution.py:11
  455.0 0.0 all-gather.4.cloned.1.call-update
  455.0 0.0 all-gather.6.cloned.1.call-start
  455.0 0.0 copy-done.1
  455.0 9.0 %fusion.14 = (bf16[2,144,4608]{2,1,0:T(8,128)(2,1)}, f32[2,144,4608]{2,1,0:T(8,128)}, f32[2,144,4608]{2,1,0:T(8,128)}) fusion(bf16[2,1152,4608]{2,1,0:T(8,128)(2,1)} %param.16, s32[]{:T(128)S(6)} %select_n.7, f32[]{:T(128)S(6)} %min_shard_map.3, bf16[2,144,4608]{2,1,0:T(8,128)(2,1)S(1)} %copy-done.1, f32[2,144,4608]{2,1,0:T(8,128)} %param.22, ...), kind=kLoop, calls=%fused_computation.29 | loop fusion | flops 22560768 | bytes 29196296 | tf_op jit(solution)/shard_map/convert_element_type | solution.py:11
  464.1 0.0 all-gather.6.cloned.1.call-update
  464.1 84.9 %all-gather.8.cloned.1.call-done = bf16[2,4608,1152]{2,1,0:T(8,128)(2,1)} async-done(((bf16[2,576,1152]{2,1,0:T(8,128)(2,1)}), bf16[2,4608,1152]{2,1,0:T(8,128)(2,1)}) %all-gather.8.cloned.1.call-update) | async-done | bytes 21233680 | tf_op jit(solution)/shard_map/all_gather | solution.py:28
  549.0 105.3 %all-gather.4.cloned.1.call-done = bf16[2,1152,4608]{2,1,0:T(8,128)(2,1)} async-done(((bf16[2,144,4608]{2,1,0:T(8,128)(2,1)}), bf16[2,1152,4608]{2,1,0:T(8,128)(2,1)}) %all-gather.4.cloned.1.call-update) | async-done | bytes 21233680 | tf_op jit(solution)/shard_map/all_gather | solution.py:28
  654.3 105.3 %all-gather.6.cloned.1.call-done = bf16[2,1152,4608]{2,1,0:T(8,128)(2,1)} async-done(((bf16[2,144,4608]{2,1,0:T(8,128)(2,1)}), bf16[2,1152,4608]{2,1,0:T(8,128)(2,1)}) %all-gather.6.cloned.1.call-update) | async-done | bytes 21233680 | tf_op jit(solution)/shard_map/all_gather | solution.py:28
  759.5 0.0 copy-start
  759.5 0.0 slice-start
  759.5 0.0 slice-start.1
  759.5 0.0 slice-start.2
  759.5 21.0 %copy.24 = bf16[2,1152,4608]{2,1,0:T(8,128)(2,1)} copy(bf16[2,1152,4608]{2,1,0:T(8,128)(2,1)} %all-gather.4.cloned.1.call-done) | data formatting | bytes 42467328
  780.5 0.0 copy-done
  780.5 0.0 slice-start.3
  780.5 0.0 slice-start.4
  780.5 0.0 slice-start.5
  780.5 10.8 %copy.25 = bf16[2,1152,4608]{2,1,0:T(8,128)(2,1)} copy(bf16[2,1152,4608]{2,1,0:T(8,128)(2,1)S(1)} %copy-done) | data formatting | bytes 42467328
  791.3 0.0 slice-done
  791.3 0.0 slice-done.1
  791.3 0.0 slice-done.2
  791.3 2.0 slice-done.3
  793.3 1.2 slice-done.4
  794.5 0.0 slice-done.5
  794.5 7.6 copy.26
  (1 shorter events, 0.0 us)
Async XLA Ops:
  7.2 135.3 %reduce-scatter.4.cloned.1.call-start = ((), (), s32[]{:S(2)}) async-start(), calls=%async_computation.3 | async-start | bytes 23887872 | tf_op jit(solution)/shard_map/reduce_scatter | solution.py:22
  7.9 266.2 %reduce-scatter.6.cloned.1.call-start = ((), (), s32[]{:S(2)}) async-start(), calls=%async_computation.4 | async-start | bytes 23887872 | tf_op jit(solution)/shard_map/reduce_scatter | solution.py:22
  8.7 397.1 %reduce-scatter.8.cloned.1.call-start = ((), (), s32[]{:S(2)}) async-start(), calls=%async_computation.5 | async-start | bytes 23887872 | tf_op jit(solution)/shard_map/reduce_scatter | solution.py:22
  9.4 539.6 %all-gather.8.cloned.1.call-start = ((), (), s32[]{:S(2)}) async-start(), calls=%async_computation.8 | async-start | bytes 23887872 | tf_op jit(solution)/shard_map/all_gather | solution.py:28
  444.0 210.3 %all-gather.4.cloned.1.call-start = ((), (), s32[]{:S(2)}) async-start(), calls=%async_computation.6 | async-start | bytes 23887872 | tf_op jit(solution)/shard_map/all_gather | solution.py:28
  444.0 11.0 %copy-start.1 = (bf16[2,144,4608]{2,1,0:T(8,128)(2,1)S(1)}, bf16[2,144,4608]{2,1,0:T(8,128)(2,1)}, u32[]{:S(2)}) copy-start(bf16[2,144,4608]{2,1,0:T(8,128)(2,1)} %reduce-scatter.6.cloned.1.call-done) | copy-start | bytes 7962628
  455.0 304.5 %all-gather.6.cloned.1.call-start = ((), (), s32[]{:S(2)}) async-start(), calls=%async_computation.7 | async-start | bytes 23887872 | tf_op jit(solution)/shard_map/all_gather | solution.py:28
  759.5 21.0 %copy-start = (bf16[2,1152,4608]{2,1,0:T(8,128)(2,1)S(1)}, bf16[2,1152,4608]{2,1,0:T(8,128)(2,1)}, u32[]{:S(2)}) copy-start(bf16[2,1152,4608]{2,1,0:T(8,128)(2,1)} %all-gather.6.cloned.1.call-done) | copy-start | bytes 63700996
  759.5 31.8 %slice-start = ((s8[21233664]{0:T(1024)(128)(4,1)}), s8[4194304]{0:T(1024)(128)(4,1)S(1)}, s32[]{:S(2)}) async-start(s8[21233664]{0:T(1024)(128)(4,1)} %bitcast.6), calls=%async_computation.9 | async-start | bytes 8388608
  759.5 31.8 %slice-start.1 = ((s8[21233664]{0:T(1024)(128)(4,1)}), s8[4194304]{0:T(1024)(128)(4,1)S(1)}, s32[]{:S(2)}) async-start(s8[21233664]{0:T(1024)(128)(4,1)} %bitcast.6), calls=%async_computation.10 | async-start | bytes 8388608
  759.5 31.8 %slice-start.2 = ((s8[21233664]{0:T(1024)(128)(4,1)}), s8[4194304]{0:T(1024)(128)(4,1)S(1)}, s32[]{:S(2)}) async-start(s8[21233664]{0:T(1024)(128)(4,1)} %bitcast.6), calls=%async_computation.11 | async-start | bytes 8388608
  780.5 12.8 %slice-start.3 = ((s8[21233664]{0:T(1024)(128)(4,1)}), s8[4194304]{0:T(1024)(128)(4,1)S(1)}, s32[]{:S(2)}) async-start(s8[21233664]{0:T(1024)(128)(4,1)} %bitcast.6), calls=%async_computation.12 | async-start | bytes 8388608
  780.5 14.0 %slice-start.4 = ((s8[21233664]{0:T(1024)(128)(4,1)}), s8[4194304]{0:T(1024)(128)(4,1)S(1)}, s32[]{:S(2)}) async-start(s8[21233664]{0:T(1024)(128)(4,1)} %bitcast.6), calls=%async_computation.13 | async-start | bytes 8388608
  780.5 14.0 %slice-start.5 = ((s8[21233664]{0:T(1024)(128)(4,1)}), s8[262144]{0:T(1024)(128)(4,1)S(1)}, s32[]{:S(2)}) async-start(s8[21233664]{0:T(1024)(128)(4,1)} %bitcast.6), calls=%async_computation.14 | async-start | bytes 524288
Sparse Core Ops, SparseCore 0:
  11.5 130.8 reduce-scatter.3
  146.0 128.0 reduce-scatter.5
  277.6 128.0 reduce-scatter.7
  444.1 104.8 all-gather.7
  551.3 102.9 all-gather.3
  656.5 102.9 all-gather.5
where the time goes:
time: 809 us
  waiting for transfers between devices  685 us (85%)
  local copies, waits for them, and re-layouts  42.6 us (5%)
  other arithmetic  42 us (5%)
  blocking collectives  22.2 us (3%)
  between operations  16.8 us (2%)
    reduce_scatter x3, waiting for transfers between devices, step(): lax.psum_scatter(t[0], 'dp', scatter_dimension=1, tiled=True)  388 us
    all_gather x3, waiting for transfers between devices, step(): whole = [lax.all_gather(one[0], 'dp', axis=1, tiled=True) for one in new]  295 us
    unnamed x19, local copies, waits for them, and re-layouts  42.6 us
    convert_element_type x3, other arithmetic, adamw(): return ((w - 0.02 * step).astype(jnp.bfloat16), m, v)  30.8 us
    psum x1, blocking collectives, step(): squares = lax.psum(sum((jnp.sum(g * g) for g in gradients)), 'dp')  22.2 us
  transfers between devices with their start and end apart: 6, of which 6 were waited for; matrix products, arithmetic and copies ran while one was open for 3% of the time, Pallas kernels for 0%

commit v1 on v0

v1 whole, which is shorter than its diff:
```python
import jax
import jax.numpy as jnp
from jax import lax
from jax.experimental import pallas as pl
from jax.experimental.pallas import tpu as pltpu
from jax.sharding import PartitionSpec as P

MESH = pl.DeviceIdType.MESH
F32, BF16 = jnp.float32, jnp.bfloat16
LAYERS, D, FF = 2, 1152, 4608
R, C, Q = 144, 1152, 4
CHUNKS = 3 * Q
STEP = 16
COUNT = LAYERS * 3 * D * FF


def chunk(ref, j, layer, d, lead=()):
    w, q = divmod(j, Q)
    if w < 2:
        return ref[w].at[*lead, layer, pl.ds(pl.multiple_of(d * R, R), R), pl.ds(q * C, C)]
    return ref[w].at[*lead, layer, pl.ds(pl.multiple_of(d * (Q * R) + q * R, R), R), :]


def own_chunk(ref, j, layer):
    w, q = divmod(j, Q)
    if w < 2:
        return ref[w].at[layer, :, pl.ds(q * C, C)]
    return ref[w].at[layer, pl.ds(q * R, R), :]


def neighbours():
    me = lax.axis_index("dp")
    x = lax.rem(me + 4, 8)
    y = me + 2 - 4 * lax.rem(me // 2, 2)
    xy = lax.rem(y + 4, 8)
    other = me + 1 - 2 * lax.rem(me, 2)
    return me, x, y, xy, other


def remote(src, dst, send, recv, to):
    return pltpu.make_async_remote_copy(src_ref=src, dst_ref=dst, send_sem=send, recv_sem=recv, device_id={"dp": to}, device_id_type=MESH)


def enter(peers):
    barrier = pltpu.get_barrier_semaphore()
    for p in peers:
        pl.semaphore_signal(barrier, inc=1, device_id={"dp": p}, device_id_type=MESH)
    pl.semaphore_wait(barrier, len(peers))


def scatter_kernel(*refs):
    g, (g_out, ss_out, landed) = refs[:3], refs[3:6]
    lo, lp, s1, s2, r1, r2, stage, acc, mine, every = refs[6:16]
    d_send, d_recv, l_sem, s1_send, r1_recv, s2_send, r2_recv, o_sem, e_send, e_recv = refs[16:]
    me, x, y, xy, other = neighbours()
    my_c = lax.rem(me, 2)
    enter([lax.rem(me + k, 8) for k in range(1, 8)])

    blocks = [me, x, y, xy]
    flip = 1 - 2 * my_c
    first = [(0, 3), (1, 3), (0, 1), (1, 2)]
    second = [(0, 2), (1, 1)]
    last = [(0, 0), (1, 0)]
    everything = first + second + last

    def swap(j, i):
        layer, k = everything[i]
        return remote(chunk(g, j, layer, blocks[k] + flip, (0,)), landed.at[j, i], d_send.at[j, i], d_recv.at[j, i], other)

    for j in range(CHUNKS):
        for i in range(8):
            swap(j, i).start()

    groups = [range(0, 4), range(4, 6), range(6, 8)]

    def loads(j, group):
        slot = j % 2
        out = []
        for i in groups[group]:
            layer, k = everything[i]
            out.append(pltpu.make_async_copy(chunk(g, j, layer, blocks[k], (0,)), lo.at[slot, i], l_sem.at[slot, i, 0]))
            out.append(pltpu.make_async_copy(landed.at[j, i], lp.at[slot, i], l_sem.at[slot, i, 1]))
        return out

    def start_loads(j, group):
        for i in groups[group]:
            swap(j, i).wait_recv()
        for c in loads(j, group):
            c.start()

    def wait_loads(j, group):
        for c in loads(j, group):
            c.wait()

    def add(dst, *terms):
        @pl.loop(0, R // STEP)
        def _(s):
            rows = pl.ds(pl.multiple_of(s * STEP, STEP), STEP)
            total = terms[0][rows, :].astype(F32)
            for t in terms[1:]:
                total = total + t[rows, :].astype(F32)
            dst[rows, :] = total.astype(BF16)

    def first_hop(j, n):
        to = (x, y, x, y)[n]
        at = (1, 3, 0, 2)[n]
        return remote(s1.at[j % 3, n], r1.at[j, at], s1_send.at[j, n], r1_recv.at[j, at], to)

    def second_hop(j, n):
        to = (y, x)[n]
        return remote(s2.at[j % 3, n], r2.at[j, n], s2_send.at[j, n], r2_recv.at[j, n], to)

    def arrived(j, at):
        n = (2, 0, 3, 1)[at]
        first_hop(j, n).wait_recv()

    def out(j, n):
        return pltpu.make_async_copy(stage.at[j % 2, n], g_out.at[n, j], o_sem.at[j % 2, n])

    acc[...] = jnp.zeros_like(acc)
    start_loads(0, 0)
    for t in range(CHUNKS + 2):
        j = t
        if j < CHUNKS:
            wait_loads(j, 0)
            if j >= 3:
                for n in range(4):
                    first_hop(j - 3, n).wait_send()
            for n in range(4):
                add(s1.at[j % 3, n], lo.at[j % 2, n], lp.at[j % 2, n])
                first_hop(j, n).start()
            if j + 1 < CHUNKS:
                start_loads(j + 1, 0)
            start_loads(j, 1)
        j = t - 1
        if 0 <= j < CHUNKS:
            wait_loads(j, 1)
            if j >= 3:
                for n in range(2):
                    second_hop(j - 3, n).wait_send()
            for n, at in ((0, 1), (1, 3)):
                arrived(j, at)
                add(s2.at[j % 3, n], lo.at[j % 2, 4 + n], lp.at[j % 2, 4 + n], r1.at[j, at])
                second_hop(j, n).start()
            start_loads(j, 2)
        j = t - 2
        if 0 <= j < CHUNKS:
            wait_loads(j, 2)
            for n, at in ((0, 0), (1, 2)):
                arrived(j, at)
                second_hop(j, n).wait_recv()
                if j >= 2:
                    out(j - 2, n).wait()
                a, b, c, e, dst = lo.at[j % 2, 6 + n], lp.at[j % 2, 6 + n], r1.at[j, at], r2.at[j, n], stage.at[j % 2, n]

                @pl.loop(0, R // STEP)
                def _(s):
                    rows = pl.ds(pl.multiple_of(s * STEP, STEP), STEP)
                    total = (a[rows, :].astype(F32) + b[rows, :].astype(F32)) + c[rows, :].astype(F32) + e[rows, :].astype(F32)
                    total = total.astype(BF16)
                    dst[rows, :] = total
                    total = total.astype(F32)
                    squares = total * total
                    acc[...] += squares[:8] + squares[8:]

                out(j, n).start()

    tile = acc[:, :128]
    for i in range(1, C // 128):
        tile = tile + acc[:, i * 128 : (i + 1) * 128]
    mine[...] = tile
    every[me] = tile
    def tell(k):
        return remote(mine, every.at[me], e_send.at[k], e_recv.at[k], lax.rem(me + k, 8))

    def told(k):
        return remote(mine, every.at[lax.rem(me + 8 - k, 8)], e_send.at[k], e_recv.at[k], lax.rem(me + k, 8))

    for k in range(1, 8):
        tell(k).start()
    for k in range(1, 8):
        told(k).wait_recv()
    total = every[0]
    for k in range(1, 8):
        total = total + every[k]
    ss_out[...] = jnp.broadcast_to(jnp.sum(total, keepdims=True), (8, 128))
    for k in range(1, 8):
        tell(k).wait_send()
    for j in range(CHUNKS):
        for i in range(8):
            swap(j, i).wait_send()
    for j in range(CHUNKS - 3, CHUNKS):
        for n in range(4):
            first_hop(j, n).wait_send()
        for n in range(2):
            second_hop(j, n).wait_send()
    for j in range(CHUNKS - 2, CHUNKS):
        for n in range(2):
            out(j, n).wait()


def scatter(terms):
    any_ = pl.BlockSpec(memory_space=pl.ANY)
    dma = pltpu.SemaphoreType.DMA
    buf = lambda *lead: pltpu.VMEM((*lead, R, C), BF16)
    return pl.pallas_call(
        scatter_kernel,
        name="scatter_sum",
        out_shape=[
            jax.ShapeDtypeStruct((2, CHUNKS, R, C), BF16),
            jax.ShapeDtypeStruct((8, 128), F32),
            jax.ShapeDtypeStruct((CHUNKS, 8, R, C), BF16),
        ],
        in_specs=[any_] * 3,
        out_specs=[any_, pl.BlockSpec(memory_space=pltpu.VMEM), any_],
        scratch_shapes=[
            buf(2, 8), buf(2, 8), buf(3, 4), buf(3, 2), buf(CHUNKS, 4), buf(CHUNKS, 2), buf(2, 2),
            pltpu.VMEM((8, C), F32), pltpu.VMEM((8, 128), F32), pltpu.VMEM((8, 8, 128), F32),
            dma((CHUNKS, 8)), dma((CHUNKS, 8)), dma((2, 8, 2)), dma((CHUNKS, 4)), dma((CHUNKS, 4)),
            dma((CHUNKS, 2)), dma((CHUNKS, 2)), dma((2, 2)), dma((8,)), dma((8,)),
        ],
        compiler_params=pltpu.CompilerParams(collective_id=0, has_side_effects=True, vmem_limit_bytes=52 * 2**20),
    )(*terms)


def adamw_kernel(me_ref, ss, g_ref, w_ref, m_ref, v_ref, new_w, new_m, new_v):
    factor = jnp.minimum(1.0, 0.5 * lax.rsqrt(ss[...] / COUNT + 1e-30))[:1, :1]

    @pl.loop(0, R // STEP)
    def _(s):
        rows = pl.ds(pl.multiple_of(s * STEP, STEP), STEP)
        g = g_ref[0, 0, rows, :].astype(F32) * factor
        w = w_ref[0, rows, :].astype(F32)
        m = 0.9 * m_ref[0, rows, :] + 0.1 * g
        v = 0.95 * v_ref[0, rows, :] + 0.05 * g * g
        step = m * lax.rsqrt(v + 1e-8) + 0.1 * w
        new_w[0, rows, :] = (w - 0.02 * step).astype(BF16)
        new_m[0, rows, :] = m
        new_v[0, rows, :] = v


def adamw(me, ss, g, which, w, m, v):
    wide = which < 2
    own = pl.BlockSpec((1, R, C), (lambda l, q, me: (l, 0, q)) if wide else (lambda l, q, me: (l, q, 0)))
    whole = pl.BlockSpec((1, R, C), (lambda l, q, me: (l, me[0], q)) if wide else (lambda l, q, me: (l, me[0] * Q + q, 0)))
    return pl.pallas_call(
        adamw_kernel,
        name=f"adamw_{which}",
        out_shape=[jax.ShapeDtypeStruct(m.shape, BF16), jax.ShapeDtypeStruct(m.shape, F32), jax.ShapeDtypeStruct(m.shape, F32)],
        grid_spec=pltpu.PrefetchScalarGridSpec(
            num_scalar_prefetch=1,
            grid=(LAYERS, Q),
            in_specs=[
                pl.BlockSpec((8, 128), lambda l, q, me: (0, 0)),
                pl.BlockSpec((1, 1, R, C), lambda l, q, me: (l, which * Q + q, 0, 0)),
                whole, own, own,
            ],
            out_specs=[own, own, own],
        ),
        compiler_params=pltpu.CompilerParams(vmem_limit_bytes=24 * 2**20),
    )(me, ss, g, w, m, v)


def gather_kernel(*refs):
    new, whole = refs[:3], refs[3:6]
    own, l_sem, o_sem, send, recv, d_send, d_recv = refs[6:]
    me, x, y, xy, other = neighbours()
    flip = 1 - 2 * lax.rem(me, 2)
    enter([x, y, other])
    blocks = [me, x, y, xy]
    every = [(layer, j) for j in range(CHUNKS) for layer in range(2)]

    def load(layer, j):
        return pltpu.make_async_copy(own_chunk(new, j, layer), own.at[layer, j], l_sem.at[layer, j])

    def store(layer, j):
        return pltpu.make_async_copy(own.at[layer, j], chunk(whole, j, layer, me), o_sem.at[layer, j])

    def hop(layer, j, h):
        if h < 2:
            src, d, to = own.at[layer, j], me, (x, y)[h]
        else:
            d = (y, x)[layer]
            src, to = chunk(whole, j, layer, d), (x, y)[layer]
        return remote(src, chunk(whole, j, layer, d), send.at[layer, j, h], recv.at[layer, j, h], to)

    def came(layer, j, h):
        d = (x, y)[h] if h < 2 else xy
        dst = chunk(whole, j, layer, d)
        return remote(dst, dst, send.at[layer, j, h], recv.at[layer, j, h], x)

    def share(layer, j, k):
        d = blocks[k]
        src = own.at[layer, j] if k == 0 else chunk(whole, j, layer, d)
        return remote(src, chunk(whole, j, layer, d), d_send.at[layer, j, k], d_recv.at[layer, j, k], other)

    def shared(layer, j, k):
        dst = chunk(whole, j, layer, blocks[k] + flip)
        return remote(dst, dst, d_send.at[layer, j, k], d_recv.at[layer, j, k], other)

    for layer, j in every:
        load(layer, j).start()
    for layer, j in every:
        load(layer, j).wait()
        hop(layer, j, 1 - layer).start()
    for layer, j in every:
        hop(layer, j, layer).start()
        share(layer, j, 0).start()
        store(layer, j).start()
    for layer, j in every:
        h = 1 - layer
        came(layer, j, h).wait_recv()
        hop(layer, j, 2).start()
        share(layer, j, 1 + h).start()
    for layer, j in every:
        came(layer, j, layer).wait_recv()
        share(layer, j, 1 + layer).start()
    for layer, j in every:
        came(layer, j, 2).wait_recv()
        share(layer, j, 3).start()
    for layer, j in every:
        store(layer, j).wait()
        for h in range(3):
            hop(layer, j, h).wait_send()
        for k in range(4):
            share(layer, j, k).wait_send()
            shared(layer, j, k).wait_recv()


def gather(new, like):
    any_ = pl.BlockSpec(memory_space=pl.ANY)
    dma = pltpu.SemaphoreType.DMA
    return pl.pallas_call(
        gather_kernel,
        name="gather",
        out_shape=[jax.ShapeDtypeStruct(w.shape, BF16) for w in like],
        in_specs=[any_] * 3,
        out_specs=[any_] * 3,
        scratch_shapes=[
            pltpu.VMEM((2, CHUNKS, R, C), BF16),
            dma((2, CHUNKS)), dma((2, CHUNKS)), dma((2, CHUNKS, 3)), dma((2, CHUNKS, 3)),
            dma((2, CHUNKS, 4)), dma((2, CHUNKS, 4)),
        ],
        compiler_params=pltpu.CompilerParams(collective_id=1, has_side_effects=True, vmem_limit_bytes=12 * 2**20),
    )(*new)


def solution(mesh):
    def step(*arrays):
        terms, weights, m, v = (arrays[i : i + 3] for i in (0, 3, 6, 9))
        g, squares, _ = scatter(terms)
        me = lax.axis_index("dp").astype(jnp.int32).reshape(1)
        new = [adamw(me, squares, g, i, weights[i], m[i], v[i]) for i in range(3)]
        whole = gather([one[0] for one in new], weights)
        return (*whole, *(one[1] for one in new), *(one[2] for one in new))

    all_of, cut = P(None, None, None), P(None, "dp", None)
    return jax.shard_map(
        step,
        mesh=mesh,
        in_specs=(P(("rep", "dp"), None, None, None),) * 3 + (all_of,) * 3 + (cut,) * 6,
        out_specs=(P("rep", None, None),) * 3 + (P("rep", "dp", None),) * 6,
        check_vma=False,
    )
```

time: 809 us -> 615 us (0.76)
  waiting for transfers between devices: 685 us -> 0 us
  Pallas kernels: 0 us -> 572 us
  other arithmetic: 42 us -> 0.01 us
  blocking collectives: 22.2 us -> 0 us
  between operations: 16.8 us -> 0.82 us
    pallas_call x0 -> x5, Pallas kernels: none -> 572 us  [the longest x1 274 us: scatter(): pl.pallas_call(scatter_kernel, name='scatter_sum', out_shape=[jax.ShapeDt...]
    reduce_scatter x3 -> x0, waiting for transfers between devices: 388 us -> none  [step(): lax.psum_scatter(t[0], 'dp', scatter_dimension=1, tiled=True)]
    all_gather x3 -> x0, waiting for transfers between devices: 295 us -> none  [step(): whole = [lax.all_gather(one[0], 'dp', axis=1, tiled=True) for one in new]]
    convert_element_type x3 -> x0, other arithmetic: 30.8 us -> none  [adamw(): return ((w - 0.02 * step).astype(jnp.bfloat16), m, v)]
    psum x1 -> x0, blocking collectives: 22.2 us -> none  [step(): squares = lax.psum(sum((jnp.sum(g * g) for g in gradients)), 'dp')]
    reduce_sum x3 -> x0, other arithmetic: 11.2 us -> none  [step(): squares = lax.psum(sum((jnp.sum(g * g) for g in gradients)), 'dp')]
    unnamed x19 -> x33, local copies, waits for them, and re-layouts: 42.6 us -> 40.9 us
  transfers between devices with their start and end apart: 6 -> 0, of which waited for: 6 -> 0; matrix products, arithmetic and copies ran while one was open for 3% -> 0% of each run, Pallas kernels for 0% -> 0%
where the time goes in v1:
time: 615 us; the launch traced here: 614 us
  Pallas kernels  572 us (93%)
  local copies, waits for them, and re-layouts  40.9 us (7%)
    pallas_call x1, Pallas kernels, scatter(): pl.pallas_call(scatter_kernel, name='scatter_sum', out_shape=[jax.ShapeDt...  274 us
    pallas_call x1, Pallas kernels, gather(): pl.pallas_call(gather_kernel, name='gather', out_shape=[jax.ShapeDtypeStr...  265 us
    unnamed x33, local copies, waits for them, and re-layouts  40.9 us
    pallas_call x3, Pallas kernels, adamw(): pl.pallas_call(adamw_kernel, name=f'adamw_{which}', out_shape=[jax.ShapeD...  33 us

profile of v1, /device:TPU:0, one launch (start us, length us, event | category | flops | bytes accessed | tf_op | source)
XLA Modules:
  0.0 614.1 jit_solution(2735082690353893590)
XLA Ops:
  0.6 0.0 copy-start.1
  0.7 0.0 copy-start.2
  0.7 274.2 %scatter_sum.1 = (bf16[2,12,144,1152]{3,2,1,0:T(8,128)(2,1)}, f32[8,128]{1,0:T(8,128)S(1)}, bf16[12,8,144,1152]{3,2,1,0:T(8,128)(2,1)}) custom-call(bf16[1,2,1152,4608]{3,2,1,0:T(8,128)(2,1)} %refs_0_.1, bf16[1,2,1152,4608]{3,2,1,0:T(8,128)(2,1)} %refs_1_.1, bf16[1,2,4608,1152]{3,2,1,0:T(8,128)(2,1)} %refs_2_.1), custom_call_target="tpu_custom_call" | custom-call | tf_op jit(solution)/shard_map/scatter_sum/pallas_call | solution.py:206
  274.9 0.0 copy-done.1
  274.9 0.0 copy-done.2
  274.9 0.0 copy-start
  274.9 3.3 copy-done
  278.2 0.0 copy-start.3
  278.2 0.0 copy-start.4
  278.2 0.0 slice-start
  278.2 0.0 slice-start.2
  278.2 12.7 %adamw_2.1 = (bf16[2,576,1152]{2,1,0:T(8,128)(2,1)S(1)}, f32[2,576,1152]{2,1,0:T(8,128)}, f32[2,576,1152]{2,1,0:T(8,128)}) custom-call(s32[1]{0:T(128)} %bitcast.me_ref, f32[8,128]{1,0:T(8,128)S(1)} %get-tuple-element.23.ss, bf16[2,12,144,1152]{3,2,1,0:T(8,128)(2,1)S(1)} %copy-done, bf16[2,4608,1152]{2,1,0:T(8,128)(2,1)} %w_ref.5, ...), custom_call_target="tpu_custom_call" | custom-call | tf_op jit(solution)/shard_map/adamw_2/pallas_call | solution.py:246
  290.9 0.0 copy-done.3
  290.9 0.0 copy-done.4
  290.9 0.0 slice-start.1
  290.9 0.0 slice-start.3
  290.9 10.2 %adamw_1.1 = (bf16[2,144,4608]{2,1,0:T(8,128)(2,1)S(1)}, f32[2,144,4608]{2,1,0:T(8,128)}, f32[2,144,4608]{2,1,0:T(8,128)}) custom-call(s32[1]{0:T(128)} %bitcast.me_ref, f32[8,128]{1,0:T(8,128)S(1)} %get-tuple-element.23.ss, bf16[2,12,144,1152]{3,2,1,0:T(8,128)(2,1)S(1)} %copy-done, bf16[2,1152,4608]{2,1,0:T(8,128)(2,1)} %w_ref.4, ...), custom_call_target="tpu_custom_call" | custom-call | tf_op jit(solution)/shard_map/adamw_1/pallas_call | solution.py:246
  301.1 0.0 slice-done
  301.1 0.0 slice-done.2
  301.1 0.0 slice-done.1
  301.1 0.0 slice-done.3
  301.1 10.1 %adamw_0.1 = (bf16[2,144,4608]{2,1,0:T(8,128)(2,1)S(1)}, f32[2,144,4608]{2,1,0:T(8,128)}, f32[2,144,4608]{2,1,0:T(8,128)}) custom-call(s32[1]{0:T(128)} %bitcast.me_ref, f32[8,128]{1,0:T(8,128)S(1)} %get-tuple-element.23.ss, bf16[2,12,144,1152]{3,2,1,0:T(8,128)(2,1)S(1)} %copy-done, bf16[2,1152,4608]{2,1,0:T(8,128)(2,1)} %w_ref.3, ...), custom_call_target="tpu_custom_call" | custom-call | tf_op jit(solution)/shard_map/adamw_0/pallas_call | solution.py:246
  311.2 265.2 %gather.1 = (bf16[2,1152,4608]{2,1,0:T(8,128)(2,1)S(1)}, bf16[2,1152,4608]{2,1,0:T(8,128)(2,1)}, bf16[2,4608,1152]{2,1,0:T(8,128)(2,1)}) custom-call(bf16[2,144,4608]{2,1,0:T(8,128)(2,1)S(1)} %get-tuple-element.25.refs_0_, bf16[2,144,4608]{2,1,0:T(8,128)(2,1)S(1)} %get-tuple-element.26.refs_1_, bf16[2,576,1152]{2,1,0:T(8,128)(2,1)S(1)} %get-tuple-element.27.refs_2_), custom_call_target="tpu_custom_call" | custom-call | tf_op jit(solution)/shard_map/gather/pallas_call | solution.py:333
  576.4 0.0 slice-start.4
  576.4 0.0 slice-start.5
  576.4 0.0 slice-start.6
  576.4 0.0 slice-start.7
  576.4 10.8 %copy.24 = bf16[2,1152,4608]{2,1,0:T(8,128)(2,1)} copy(bf16[2,1152,4608]{2,1,0:T(8,128)(2,1)S(1)} %get-tuple-element.46) | data formatting | bytes 42467328
  587.2 0.0 slice-start.8
  587.2 0.0 slice-start.9
  587.2 19.2 %copy.25 = bf16[2,1152,4608]{2,1,0:T(8,128)(2,1)} copy(bf16[2,1152,4608]{2,1,0:T(8,128)(2,1)} %get-tuple-element.47) | data formatting | bytes 42467328
  606.4 0.0 slice-done.4
  606.4 0.0 slice-done.5
  606.4 0.0 slice-done.6
  606.4 0.0 slice-done.7
  606.4 0.0 slice-done.8
  606.4 0.0 slice-done.9
  606.4 7.6 %copy.26 = bf16[2,4608,1152]{2,1,0:T(8,128)(2,1)} copy(bf16[2,4608,1152]{2,1,0:T(8,128)(2,1)S(1)} %bitcast.6) | data formatting | bytes 42467328
  (3 shorter events, 0.0 us)
Async XLA Ops:
  0.6 274.2 %copy-start.1 = (f32[2,576,1152]{2,1,0:T(8,128)S(1)}, f32[2,576,1152]{2,1,0:T(8,128)}, u32[]{:S(2)}) copy-start(f32[2,576,1152]{2,1,0:T(8,128)} %m_ref.5) | copy-start | bytes 15925252
  0.7 274.2 %copy-start.2 = (f32[2,576,1152]{2,1,0:T(8,128)S(1)}, f32[2,576,1152]{2,1,0:T(8,128)}, u32[]{:S(2)}) copy-start(f32[2,576,1152]{2,1,0:T(8,128)} %v_ref.5) | copy-start | bytes 15925252
  274.9 3.3 copy-start
  278.2 12.7 %copy-start.3 = (f32[2,144,4608]{2,1,0:T(8,128)S(1)}, f32[2,144,4608]{2,1,0:T(8,128)}, u32[]{:S(2)}) copy-start(f32[2,144,4608]{2,1,0:T(8,128)} %m_ref.4) | copy-start | bytes 15925252
  278.2 12.7 %copy-start.4 = (f32[2,144,4608]{2,1,0:T(8,128)S(1)}, f32[2,144,4608]{2,1,0:T(8,128)}, u32[]{:S(2)}) copy-start(f32[2,144,4608]{2,1,0:T(8,128)} %v_ref.4) | copy-start | bytes 15925252
  278.2 22.9 %slice-start = ((s8[5308416]{0:T(1024)(128)(4,1)}), s8[4194304]{0:T(1024)(128)(4,1)S(1)}, s32[]{:S(2)}) async-start(s8[5308416]{0:T(1024)(128)(4,1)} %bitcast.1), calls=%async_computation | async-start | bytes 8388608
  278.2 22.9 %slice-start.2 = ((s8[5308416]{0:T(1024)(128)(4,1)}), s8[1114112]{0:T(1024)(128)(4,1)S(1)}, s32[]{:S(2)}) async-start(s8[5308416]{0:T(1024)(128)(4,1)} %bitcast.3), calls=%async_computation.2 | async-start | bytes 2228224
  290.9 10.2 %slice-start.1 = ((s8[5308416]{0:T(1024)(128)(4,1)}), s8[1114112]{0:T(1024)(128)(4,1)S(1)}, s32[]{:S(2)}) async-start(s8[5308416]{0:T(1024)(128)(4,1)} %bitcast.1), calls=%async_computation.1 | async-start | bytes 2228224
  290.9 10.2 %slice-start.3 = ((s8[5308416]{0:T(1024)(128)(4,1)}), s8[4194304]{0:T(1024)(128)(4,1)S(1)}, s32[]{:S(2)}) async-start(s8[5308416]{0:T(1024)(128)(4,1)} %bitcast.3), calls=%async_computation.3 | async-start | bytes 8388608
  576.4 30.0 %slice-start.4 = ((s8[21233664]{0:T(1024)(128)(4,1)}), s8[262144]{0:T(1024)(128)(4,1)S(1)}, s32[]{:S(2)}) async-start(s8[21233664]{0:T(1024)(128)(4,1)} %bitcast.5), calls=%async_computation.4 | async-start | bytes 524288
  576.4 30.0 %slice-start.5 = ((s8[21233664]{0:T(1024)(128)(4,1)}), s8[4194304]{0:T(1024)(128)(4,1)S(1)}, s32[]{:S(2)}) async-start(s8[21233664]{0:T(1024)(128)(4,1)} %bitcast.5), calls=%async_computation.5 | async-start | bytes 8388608
  576.4 30.0 %slice-start.6 = ((s8[21233664]{0:T(1024)(128)(4,1)}), s8[4194304]{0:T(1024)(128)(4,1)S(1)}, s32[]{:S(2)}) async-start(s8[21233664]{0:T(1024)(128)(4,1)} %bitcast.5), calls=%async_computation.6 | async-start | bytes 8388608
  576.4 30.0 %slice-start.7 = ((s8[21233664]{0:T(1024)(128)(4,1)}), s8[4194304]{0:T(1024)(128)(4,1)S(1)}, s32[]{:S(2)}) async-start(s8[21233664]{0:T(1024)(128)(4,1)} %bitcast.5), calls=%async_computation.7 | async-start | bytes 8388608
  587.2 19.3 %slice-start.8 = ((s8[21233664]{0:T(1024)(128)(4,1)}), s8[4194304]{0:T(1024)(128)(4,1)S(1)}, s32[]{:S(2)}) async-start(s8[21233664]{0:T(1024)(128)(4,1)} %bitcast.5), calls=%async_computation.8 | async-start | bytes 8388608
  587.2 19.3 %slice-start.9 = ((s8[21233664]{0:T(1024)(128)(4,1)}), s8[4194304]{0:T(1024)(128)(4,1)S(1)}, s32[]{:S(2)}) async-start(s8[21233664]{0:T(1024)(128)(4,1)} %bitcast.5), calls=%async_computation.9 | async-start | bytes 8388608
